TPU v7x, 32 devices: a whole 2x2x4 slice. The times are simulated.
32 devices in a mesh: gx: 8 (over y, x, core), gy: 4 (over z).
Axes of the slice: x: 2, y: 2, z: 4, core: 2. Of those that a mesh axis runs over, the one named last changes fastest.
Arguments:
- rhs_conc: float32 [16, 64, 2048], P('gx', 'gy'), may hold values from -60 to 60
- rhs_pots: float32 [16, 64, 33], P('gx', 'gy'), may hold values from -60 to 60
- diffusion: float32 [16, 64, 32], P('gx', 'gy'), may hold values from 0.05 to 5
- exchange: float32 [16, 64, 32], P('gx', 'gy'), may hold values from 0.2 to 4
- slope: float32 [16, 64, 32], P('gx', 'gy'), may hold values from 0.1 to 1
Outputs:
- sol_conc: float32 [16, 64, 2048], P('gx', 'gy')
- sol_pots: float32 [16, 64, 33], P('gx', 'gy')
All inputs are finite; a program needn't handle non-finite values.
Results may differ from a plain program's by a relative error of at most 0.0003.
Values sent between devices are 32-bit elements; how exact they have to be, the bound alone decides.
No kernel may reach another device: no remote copies, remote signals or barrier semaphores. Data moves between devices by JAX's collectives and lax.ppermute only.
A program may use at most 64 MiB of HBM per device.

v0:
```python
import jax
import jax.numpy as jnp
from jax import lax
from jax.sharding import PartitionSpec as P

ITERS = 10
node_cond = 1.0
plane_cond = 0.5
collector_cond = 2.0
epsilon = 1e-06


def padded_2(cells, sides, width):
    for axis, dim in sides:
        count = lax.axis_size(axis)
        ends = count - 1
        head = lax.slice_in_dim(cells, 0, width, axis=dim)
        tail = lax.slice_in_dim(cells, cells.shape[dim] - width, cells.shape[dim], axis=dim)
        cells = jnp.concatenate(
            [
                lax.ppermute(tail, axis, [(i, (i + 1) % count) for i in range(ends)]),
                cells,
                lax.ppermute(head, axis, [((i + 1) % count, i) for i in range(ends)]),
            ],
            axis=dim,
        )
    return cells


def mirror_laplace(values):
    inner = jnp.concatenate([values[..., :1], values[..., :-1]], axis=-1)
    outer = jnp.concatenate([values[..., 1:], values[..., -1:]], axis=-1)
    return 2.0 * values - inner - outer


def local_operator(conc, padded, diffusion, exchange, slope):
    nodes = exchange.shape[2]
    shell_count = conc.shape[2] // nodes
    shells = conc.reshape(conc.shape[0], conc.shape[1], nodes, shell_count)
    center = padded[1:-1, 1:-1]
    lateral = (
        4.0 * center - padded[2:, 1:-1] - padded[:-2, 1:-1] - padded[1:-1, 2:] - padded[1:-1, :-2]
    )
    node_pot = center[..., :nodes]
    collector = center[..., nodes]
    current = exchange * (node_pot - collector[..., None])
    surface = shells[..., shell_count - 1]
    surface_flag = (lax.broadcasted_iota(jnp.int32, (shell_count,), 0) == shell_count - 1).astype(
        jnp.float32
    )
    new_shells = (
        shells + diffusion[..., None] * mirror_laplace(shells) + current[..., None] * surface_flag
    )
    new_nodes = (
        node_cond * mirror_laplace(node_pot)
        + current
        - slope * surface
        + plane_cond * lateral[..., :nodes]
    )
    new_collector = collector_cond * lateral[..., nodes] - jnp.mean(current, axis=-1)
    return (
        new_shells.reshape(conc.shape),
        jnp.concatenate([new_nodes, new_collector[..., None]], axis=-1),
    )


def least_squares(columns, start_norm):
    count = len(columns)
    target = [start_norm] + [jnp.zeros_like(start_norm) for step in range(count)]
    cosines = []
    sines = []
    upper_rows = []
    for step in range(count):
        entries = list(columns[step])
        for row in range(step):
            first = cosines[row] * entries[row] + sines[row] * entries[row + 1]
            second = cosines[row] * entries[row + 1] - sines[row] * entries[row]
            entries[row] = first
            entries[row + 1] = second
        radius = jnp.sqrt(entries[step] * entries[step] + entries[step + 1] * entries[step + 1])
        cosine = entries[step] / radius
        sine = entries[step + 1] / radius
        entries[step] = radius
        cosines.append(cosine)
        sines.append(sine)
        lead = target[step]
        target[step] = cosine * lead
        target[step + 1] = -sine * lead
        upper_rows.append(entries[: step + 1])
    weights = [None] * count
    for row in range(count - 1, -1, -1):
        total = target[row]
        for later in range(row + 1, count):
            total = total - upper_rows[later][row] * weights[later]
        weights[row] = total / upper_rows[row][row]
    return weights


def shards(rhs_conc, rhs_pots, diffusion, exchange, slope):
    local_square = jnp.sum(rhs_conc * rhs_conc) + jnp.sum(rhs_pots * rhs_pots)
    start_norm = jnp.sqrt(lax.psum(local_square, ("gx", "gy")) + epsilon)
    basis = [(rhs_conc / start_norm, rhs_pots / start_norm)]
    columns = []
    for step in range(ITERS):
        padded = padded_2(basis[step][1], (("gx", 0), ("gy", 1)), 1)
        image_conc, image_pots = local_operator(basis[step][0], padded, diffusion, exchange, slope)
        local_dots = jnp.stack(
            [jnp.sum(vector[0] * image_conc) + jnp.sum(vector[1] * image_pots) for vector in basis]
        )
        image_square = jnp.sum(image_conc * image_conc) + jnp.sum(image_pots * image_pots)
        coeffs, total_square = lax.psum((local_dots, image_square), ("gx", "gy"))
        rest_conc, rest_pots = (image_conc, image_pots)
        for row in range(step + 1):
            rest_conc = rest_conc - coeffs[row] * basis[row][0]
            rest_pots = rest_pots - coeffs[row] * basis[row][1]
        height = jnp.sqrt(total_square - jnp.sum(coeffs * coeffs) + epsilon)
        basis.append((rest_conc / height, rest_pots / height))
        columns.append([coeffs[row] for row in range(step + 1)] + [height])
    weights = least_squares(columns, start_norm)
    sol_conc = weights[0] * basis[0][0]
    sol_pots = weights[0] * basis[0][1]
    for step in range(1, ITERS):
        sol_conc = sol_conc + weights[step] * basis[step][0]
        sol_pots = sol_pots + weights[step] * basis[step][1]
    return (sol_conc, sol_pots)


def solution(mesh):
    return jax.shard_map(
        shards,
        mesh=mesh,
        in_specs=(
            P("gx", "gy", None),
            P("gx", "gy", None),
            P("gx", "gy", None),
            P("gx", "gy", None),
            P("gx", "gy", None),
        ),
        out_specs=(P("gx", "gy", None), P("gx", "gy", None)),
        check_vma=False,
    )
```

profile of v0, /device:TPU:0, one launch (start us, length us, event | category | flops | bytes accessed | tf_op | source)
XLA Modules:
  0.0 950.6 jit_solution(5201951569017878183)
XLA Ops:
  5.1 42.0 %psum.147 = f32[]{:T(128)} all-reduce(f32[]{:T(128)S(6)} %add.632), channel_id=1, replica_groups=mesh['gx'=8,'gy'=4] {'gx','gy'}, use_global_device_ids=true, to_apply=%region_2.0 | all-reduce | flops 1 | bytes 8 | tf_op jit(solution)/shard_map/psum | solution.py:101
  49.2 3.0 collective-permute-start.1
  57.7 4.5 collective-permute-start.3
  69.2 42.0 %all-reduce.9 = (f32[]{:T(128)}, f32[1]{0:T(128)}) all-reduce(f32[]{:T(128)S(6)} %add.639, f32[1]{0:T(128)} %bitcast.3), channel_id=1, replica_groups=mesh['gx'=8,'gy'=4] {'gx','gy'}, use_global_device_ids=true, to_apply=%region_9.0 | all-reduce | flops 2 | bytes 16 | tf_op jit(solution)/shard_map/psum | solution.py:111
  116.6 3.0 collective-permute-start.5
  124.6 4.5 collective-permute-start.7
  137.5 42.3 %all-reduce.8 = (f32[]{:T(128)}, f32[2]{0:T(128)S(1)}) all-reduce(f32[]{:T(128)S(6)} %add.649, f32[2]{0:T(128)S(1)} %pad_maximum_fusion.120), channel_id=1, replica_groups=mesh['gx'=8,'gy'=4] {'gx','gy'}, use_global_device_ids=true, to_apply=%region_18.0 | all-reduce | flops 3 | bytes 24 | tf_op jit(solution)/shard_map/psum | solution.py:111
  187.5 3.0 collective-permute-start.9
  196.1 4.7 collective-permute-start.11
  210.8 41.6 %all-reduce.7 = (f32[]{:T(128)}, f32[3]{0:T(128)S(1)}) all-reduce(f32[]{:T(128)S(6)} %add.660, f32[3]{0:T(128)S(1)} %pad_maximum_fusion.121), channel_id=1, replica_groups=mesh['gx'=8,'gy'=4] {'gx','gy'}, use_global_device_ids=true, to_apply=%region_30.0 | all-reduce | flops 4 | bytes 32 | tf_op jit(solution)/shard_map/psum | solution.py:111
  262.0 3.0 collective-permute-start.13
  271.7 4.5 collective-permute-start.15
  287.7 41.9 %all-reduce.6 = (f32[]{:T(128)}, f32[4]{0:T(128)S(1)}) all-reduce(f32[]{:T(128)S(6)} %add.672, f32[4]{0:T(128)S(1)} %pad_maximum_fusion.122), channel_id=1, replica_groups=mesh['gx'=8,'gy'=4] {'gx','gy'}, use_global_device_ids=true, to_apply=%region_44.0 | all-reduce | flops 5 | bytes 40 | tf_op jit(solution)/shard_map/psum | solution.py:111
  332.2 2.6 subtract_divide_fusion.14
  336.7 2.7 subtract_divide_fusion.5
  341.3 3.0 collective-permute-start.17
  353.1 4.5 collective-permute-start.19
  370.5 41.6 %all-reduce.5 = (f32[]{:T(128)}, f32[5]{0:T(128)S(1)}) all-reduce(f32[]{:T(128)S(6)} %add.685, f32[5]{0:T(128)S(1)} %stack.210), channel_id=1, replica_groups=mesh['gx'=8,'gy'=4] {'gx','gy'}, use_global_device_ids=true, to_apply=%region_60.0 | all-reduce | flops 6 | bytes 48 | tf_op jit(solution)/shard_map/psum | solution.py:111
  414.7 3.2 subtract_divide_fusion.13
  419.1 3.2 subtract_divide_fusion.4
  424.3 3.2 collective-permute-start.21
  438.2 4.5 collective-permute-start.23
  456.9 41.9 %all-reduce.4 = (f32[]{:T(128)}, f32[6]{0:T(128)S(1)}) all-reduce(f32[]{:T(128)S(6)} %add.699, f32[6]{0:T(128)S(1)} %stack.217), channel_id=1, replica_groups=mesh['gx'=8,'gy'=4] {'gx','gy'}, use_global_device_ids=true, to_apply=%region_78.0 | all-reduce | flops 7 | bytes 56 | tf_op jit(solution)/shard_map/psum | solution.py:111
  501.4 3.7 subtract_divide_fusion.12
  506.9 3.8 subtract_divide_fusion.3
  515.4 3.0 collective-permute-start.25
  530.8 4.5 collective-permute-start.27
  551.5 41.6 %all-reduce.3 = (f32[]{:T(128)}, f32[7]{0:T(128)S(1)}) all-reduce(f32[]{:T(128)S(6)} %add.714, f32[7]{0:T(128)S(1)} %stack.225), channel_id=1, replica_groups=mesh['gx'=8,'gy'=4] {'gx','gy'}, use_global_device_ids=true, to_apply=%region_98.0 | all-reduce | flops 8 | bytes 64 | tf_op jit(solution)/shard_map/psum | solution.py:111
  595.8 4.4 subtract_divide_fusion.11
  602.2 4.5 subtract_divide_fusion.2
  611.8 2.1 copy.529
  615.2 3.6 collective-permute-start.29
  618.8 2.1 pad_maximum_fusion.15
  632.6 4.8 collective-permute-start.31
  645.6 2.6 multiply_reduce_fusion.22
  659.6 40.8 %all-reduce.2 = (f32[]{:T(128)}, f32[8]{0:T(128)S(1)}) all-reduce(f32[]{:T(128)S(6)} %add.730, f32[8]{0:T(128)S(1)} %stack.234), channel_id=1, replica_groups=mesh['gx'=8,'gy'=4] {'gx','gy'}, use_global_device_ids=true, to_apply=%region_120.0 | all-reduce | flops 9 | bytes 72 | tf_op jit(solution)/shard_map/psum | solution.py:111
  703.1 5.0 subtract_divide_fusion.10
  710.7 5.1 subtract_divide_fusion.1
  723.4 2.1 copy.530
  726.8 3.6 collective-permute-start.33
  730.4 2.1 pad_maximum_fusion.17
  743.7 4.5 collective-permute-start.35
  772.0 41.0 %all-reduce.1 = (f32[]{:T(128)}, f32[9]{0:T(128)S(1)}) all-reduce(f32[]{:T(128)S(6)} %add.747, f32[9]{0:T(128)S(1)} %stack.244), channel_id=1, replica_groups=mesh['gx'=8,'gy'=4] {'gx','gy'}, use_global_device_ids=true, to_apply=%region_144.0 | all-reduce | flops 10 | bytes 80 | tf_op jit(solution)/shard_map/psum | solution.py:111
  815.7 5.7 subtract_divide_fusion.9
  824.0 6.6 subtract_divide_fusion
  843.1 3.6 collective-permute-start.37
  861.6 4.5 collective-permute-start.39
  891.7 40.8 %all-reduce = (f32[10]{0:T(128)S(1)}, f32[]{:T(128)}) all-reduce(f32[10]{0:T(128)S(1)} %stack.255, f32[]{:T(128)S(6)} %add.765), channel_id=1, replica_groups=mesh['gx'=8,'gy'=4] {'gx','gy'}, use_global_device_ids=true, to_apply=%region_167.0 | all-reduce | flops 11 | bytes 88 | tf_op jit(solution)/shard_map/psum | solution.py:111
  (508 shorter events, 182.0 us)
Async XLA Ops:
  2.0 50.2 %copy-start = (f32[2,16,2048]{2,1,0:T(8,128)S(1)}, f32[2,16,2048]{2,1,0:T(8,128)}, u32[]{:S(2)}) copy-start(f32[2,16,2048]{2,1,0:T(8,128)} %param.5) | copy-start | bytes 786436
  47.9 8.4 collective-permute-start
  49.2 7.1 collective-permute-start.1
  56.4 6.2 collective-permute-start.2
  57.7 6.5 collective-permute-start.3
  115.3 7.8 collective-permute-start.4
  116.6 6.5 collective-permute-start.5
  123.3 6.2 collective-permute-start.6
  124.6 6.5 collective-permute-start.7
  186.2 8.4 collective-permute-start.8
  187.5 7.1 collective-permute-start.9
  194.8 6.4 collective-permute-start.10
  196.1 6.5 collective-permute-start.11
  260.7 9.5 collective-permute-start.12
  262.0 8.2 collective-permute-start.13
  270.4 6.2 collective-permute-start.14
  271.7 6.5 collective-permute-start.15
  340.0 11.7 %collective-permute-start.16 = (f32[1,16,33]{1,0,2:T(1,128)}, f32[1,16,33]{1,0,2:T(1,128)S(1)}, u32[]{:S(2)}, u32[]{:S(2)}) collective-permute-start(f32[1,16,33]{1,0,2:T(1,128)} %get-tuple-element.304), channel_id=1, source_target_pairs={{4,0},{8,4},{12,8},{16,12},{20,16},{24,20},{28,24},{5,1},{9,5},{13... | collective-permute-start | bytes 6344 | tf_op jit(solution)/shard_map/ppermute | solution.py:23
  341.3 10.4 %collective-permute-start.17 = (f32[1,16,33]{1,0,2:T(1,128)}, f32[1,16,33]{1,0,2:T(1,128)S(1)}, u32[]{:S(2)}, u32[]{:S(2)}) collective-permute-start(f32[1,16,33]{1,0,2:T(1,128)} %get-tuple-element.303), channel_id=1, source_target_pairs={{0,4},{4,8},{8,12},{12,16},{16,20},{20,24},{24,28},{1,5},{5,9},{9,... | collective-permute-start | bytes 6344 | tf_op jit(solution)/shard_map/ppermute | solution.py:21
  351.8 6.2 collective-permute-start.18
  353.1 6.5 collective-permute-start.19
  423.0 13.7 %collective-permute-start.20 = (f32[1,16,33]{1,0,2:T(1,128)S(1)}, f32[1,16,33]{1,0,2:T(1,128)S(1)}, u32[]{:S(2)}, u32[]{:S(2)}) collective-permute-start(f32[1,16,33]{1,0,2:T(1,128)S(1)} %get-tuple-element.297), channel_id=1, source_target_pairs={{4,0},{8,4},{12,8},{16,12},{20,16},{24,20},{28,24},{5,1},{9,5},{13... | collective-permute-start | bytes 6344 | tf_op jit(solution)/shard_map/ppermute | solution.py:23
  424.3 12.4 %collective-permute-start.21 = (f32[1,16,33]{1,0,2:T(1,128)S(1)}, f32[1,16,33]{1,0,2:T(1,128)S(1)}, u32[]{:S(2)}, u32[]{:S(2)}) collective-permute-start(f32[1,16,33]{1,0,2:T(1,128)S(1)} %get-tuple-element.296), channel_id=1, source_target_pairs={{0,4},{4,8},{8,12},{12,16},{16,20},{20,24},{24,28},{1,5},{5,9},{9,... | collective-permute-start | bytes 6344 | tf_op jit(solution)/shard_map/ppermute | solution.py:21
  436.9 6.2 collective-permute-start.22
  438.2 6.5 collective-permute-start.23
  514.1 15.2 %collective-permute-start.24 = (f32[1,16,33]{1,0,2:T(1,128)}, f32[1,16,33]{1,0,2:T(1,128)S(1)}, u32[]{:S(2)}, u32[]{:S(2)}) collective-permute-start(f32[1,16,33]{1,0,2:T(1,128)} %get-tuple-element.289), channel_id=1, source_target_pairs={{4,0},{8,4},{12,8},{16,12},{20,16},{24,20},{28,24},{5,1},{9,5},{13... | collective-permute-start | bytes 6344 | tf_op jit(solution)/shard_map/ppermute | solution.py:23
  515.4 13.9 %collective-permute-start.25 = (f32[1,16,33]{1,0,2:T(1,128)}, f32[1,16,33]{1,0,2:T(1,128)S(1)}, u32[]{:S(2)}, u32[]{:S(2)}) collective-permute-start(f32[1,16,33]{1,0,2:T(1,128)} %get-tuple-element.288), channel_id=1, source_target_pairs={{0,4},{4,8},{8,12},{12,16},{16,20},{20,24},{24,28},{1,5},{5,9},{9,... | collective-permute-start | bytes 6344 | tf_op jit(solution)/shard_map/ppermute | solution.py:21
  529.5 6.2 collective-permute-start.26
  530.8 6.5 collective-permute-start.27
  609.2 9.5 %copy-start.3 = (f32[2,16,32,1]{3,2,1,0:T(8,128)S(1)}, f32[2,16,32,1]{3,2,1,0:T(8,128)}, u32[]{:S(2)}) copy-start(f32[2,16,32,1]{3,2,1,0:T(8,128)} %get-tuple-element.197) | copy-start | bytes 12292
  613.9 16.6 %collective-permute-start.28 = (f32[1,16,33]{1,0,2:T(1,128)}, f32[1,16,33]{1,0,2:T(1,128)S(1)}, u32[]{:S(2)}, u32[]{:S(2)}) collective-permute-start(f32[1,16,33]{1,0,2:T(1,128)} %get-tuple-element.280), channel_id=1, source_target_pairs={{4,0},{8,4},{12,8},{16,12},{20,16},{24,20},{28,24},{5,1},{9,5},{13... | collective-permute-start | bytes 6344 | tf_op jit(solution)/shard_map/ppermute | solution.py:23
  615.2 15.3 %collective-permute-start.29 = (f32[1,16,33]{1,0,2:T(1,128)}, f32[1,16,33]{1,0,2:T(1,128)}, u32[]{:S(2)}, u32[]{:S(2)}) collective-permute-start(f32[1,16,33]{1,0,2:T(1,128)} %get-tuple-element.279), channel_id=1, source_target_pairs={{0,4},{4,8},{8,12},{12,16},{16,20},{20,24},{24,28},{1,5},{5,9},{9,... | collective-permute-start | bytes 6344 | tf_op jit(solution)/shard_map/ppermute | solution.py:21
  621.9 7.6 copy-start.8
  631.3 7.2 collective-permute-start.30
  632.6 7.0 collective-permute-start.31
  703.1 7.6 copy-start.19
  718.4 12.0 %copy-start.2 = (f32[2,16,32,1]{3,2,1,0:T(8,128)S(1)}, f32[2,16,32,1]{3,2,1,0:T(8,128)}, u32[]{:S(2)}) copy-start(f32[2,16,32,1]{3,2,1,0:T(8,128)} %get-tuple-element.193) | copy-start | bytes 12292
  725.5 16.0 %collective-permute-start.32 = (f32[1,16,33]{1,0,2:T(1,128)}, f32[1,16,33]{1,0,2:T(1,128)}, u32[]{:S(2)}, u32[]{:S(2)}) collective-permute-start(f32[1,16,33]{1,0,2:T(1,128)} %get-tuple-element.270), channel_id=1, source_target_pairs={{4,0},{8,4},{12,8},{16,12},{20,16},{24,20},{28,24},{5,1},{9,5},{13... | collective-permute-start | bytes 6344 | tf_op jit(solution)/shard_map/ppermute | solution.py:23
  726.8 14.7 %collective-permute-start.33 = (f32[1,16,33]{1,0,2:T(1,128)}, f32[1,16,33]{1,0,2:T(1,128)}, u32[]{:S(2)}, u32[]{:S(2)}) collective-permute-start(f32[1,16,33]{1,0,2:T(1,128)} %get-tuple-element.269), channel_id=1, source_target_pairs={{0,4},{4,8},{8,12},{12,16},{16,20},{20,24},{24,28},{1,5},{5,9},{9,... | collective-permute-start | bytes 6344 | tf_op jit(solution)/shard_map/ppermute | solution.py:21
  733.6 7.0 copy-start.7
  742.4 7.7 collective-permute-start.34
  743.7 7.0 collective-permute-start.35
  771.9 43.8 %copy-start.24 = (f32[2,16,32]{1,0,2:T(2,128)S(1)}, f32[2,16,32]{1,0,2:T(2,128)}, u32[]{:S(2)}) copy-start(f32[2,16,32]{1,0,2:T(2,128)} %get-tuple-element.161) | copy-start | bytes 12292
  834.1 12.7 %copy-start.1 = (f32[2,16,32,1]{3,2,1,0:T(8,128)S(1)}, f32[2,16,32,1]{3,2,1,0:T(8,128)}, u32[]{:S(2)}) copy-start(f32[2,16,32,1]{3,2,1,0:T(8,128)} %get-tuple-element.189) | copy-start | bytes 12292
  841.9 17.0 %collective-permute-start.36 = (f32[1,16,33]{1,0,2:T(1,128)}, f32[1,16,33]{1,0,2:T(1,128)}, u32[]{:S(2)}, u32[]{:S(2)}) collective-permute-start(f32[1,16,33]{1,0,2:T(1,128)} %get-tuple-element.259), channel_id=1, source_target_pairs={{4,0},{8,4},{12,8},{16,12},{20,16},{24,20},{28,24},{5,1},{9,5},{13... | collective-permute-start | bytes 6344 | tf_op jit(solution)/shard_map/ppermute | solution.py:23
  843.1 15.7 %collective-permute-start.37 = (f32[1,16,33]{1,0,2:T(1,128)}, f32[1,16,33]{1,0,2:T(1,128)}, u32[]{:S(2)}, u32[]{:S(2)}) collective-permute-start(f32[1,16,33]{1,0,2:T(1,128)} %get-tuple-element.258), channel_id=1, source_target_pairs={{0,4},{4,8},{8,12},{12,16},{16,20},{20,24},{24,28},{1,5},{5,9},{9,... | collective-permute-start | bytes 6344 | tf_op jit(solution)/shard_map/ppermute | solution.py:21
  860.3 7.7 collective-permute-start.38
  861.6 7.0 collective-permute-start.39
  (55 other events, 91.8 us)
where the time goes:
time: 965 us; the launch traced here: 951 us
  blocking collectives  457 us (47%)
  between operations  171 us (18%)
  other arithmetic  118 us (12%)
  starting transfers between devices  104 us (11%)
  local copies, waits for them, and re-layouts  87.2 us (9%)
  waiting for transfers between devices  12.9 us (1%)
    psum x10, blocking collectives, shards(): coeffs, total_square = lax.psum((local_dots, image_square), ('gx', 'gy'))  415 us
    ppermute x20, starting transfers between devices, padded_2(): lax.ppermute(tail, axis, [(i, (i + 1) % count) for i in range(ends)])  78.2 us
    div x18, other arithmetic, shards(): basis.append((rest_conc / height, rest_pots / height))  58.3 us
    psum x1, blocking collectives, shards(): start_norm = jnp.sqrt(lax.psum(local_square, ('gx', 'gy')) + epsilon)  42 us
    ppermute x20, starting transfers between devices, padded_2(): lax.ppermute(head, axis, [((i + 1) % count, i) for i in range(ends)])  25.8 us
  transfers between devices with their start and end apart: 40, of which 10 were waited for; matrix products, arithmetic and copies ran while one was open for 4% of the time, Pallas kernels for 0%

commit v1 on v0

--- a/solution.py
+++ b/solution.py
@@ -108,7 +108,11 @@
             [jnp.sum(vector[0] * image_conc) + jnp.sum(vector[1] * image_pots) for vector in basis]
         )
         image_square = jnp.sum(image_conc * image_conc) + jnp.sum(image_pots * image_pots)
-        coeffs, total_square = lax.psum((local_dots, image_square), ("gx", "gy"))
+
+        def masks_fix(message):
+            return jax.lax.psum(jax.lax.psum(message, "gx"), "gy")
+
+        coeffs, total_square = masks_fix((local_dots, image_square))
         rest_conc, rest_pots = (image_conc, image_pots)
         for row in range(step + 1):
             rest_conc = rest_conc - coeffs[row] * basis[row][0]

time: 965 us -> 793 us (0.82)
  blocking collectives: 457 us -> 283 us
    psum x10 -> x20, blocking collectives: 415 us -> 241 us  [masks_fix(): return jax.lax.psum(jax.lax.psum(message, 'gx'), 'gy')]
  transfers between devices with their start and end apart: 40 -> 40, of which waited for: 10 -> 15; matrix products, arithmetic and copies ran while one was open for 4% -> 5% of each run, Pallas kernels for 0% -> 0%
where the time goes in v1:
time: 793 us; the launch traced here: 777 us
  blocking collectives  283 us (36%)
  between operations  171 us (22%)
  other arithmetic  118 us (15%)
  starting transfers between devices  104 us (13%)
  local copies, waits for them, and re-layouts  87.2 us (11%)
  waiting for transfers between devices  14.8 us (2%)
    psum x20, blocking collectives, masks_fix(): return jax.lax.psum(jax.lax.psum(message, 'gx'), 'gy')  241 us
    ppermute x20, starting transfers between devices, padded_2(): lax.ppermute(tail, axis, [(i, (i + 1) % count) for i in range(ends)])  77.8 us
    div x18, other arithmetic, shards(): basis.append((rest_conc / height, rest_pots / height))  58.3 us
    psum x1, blocking collectives, shards(): start_norm = jnp.sqrt(lax.psum(local_square, ('gx', 'gy')) + epsilon)  42 us
    ppermute x20, starting transfers between devices, padded_2(): lax.ppermute(head, axis, [((i + 1) % count, i) for i in range(ends)])  25.8 us
    unnamed x139, local copies, waits for them, and re-layouts  18.5 us
  transfers between devices with their start and end apart: 40, of which 15 were waited for; matrix products, arithmetic and copies ran while one was open for 5% of the time, Pallas kernels for 0%

profile of v1, /device:TPU:0, one launch (start us, length us, event | category | flops | bytes accessed | tf_op | source)
XLA Modules:
  0.0 777.4 jit_solution(15092700923045847980)
XLA Ops:
  5.1 42.0 %psum.287 = f32[]{:T(128)} all-reduce(f32[]{:T(128)S(6)} %add.672), channel_id=1, replica_groups=mesh['gx'=8,'gy'=4] {'gx','gy'}, use_global_device_ids=true, to_apply=%region_2.0 | all-reduce | flops 1 | bytes 8 | tf_op jit(solution)/shard_map/psum | solution.py:101
  49.2 3.0 collective-permute-start.1
  57.7 4.5 collective-permute-start.3
  69.2 13.7 %all-reduce.9 = (f32[]{:T(128)}, f32[1]{0:T(128)}) all-reduce(f32[]{:T(128)S(6)} %add.679, f32[1]{0:T(128)} %bitcast.3), channel_id=1, replica_groups=mesh['gx'=8,'gy'=4] {'gx'}, use_global_device_ids=true, to_apply=%region_10.0 | all-reduce | flops 2 | bytes 16 | tf_op jit(solution)/shard_map/psum | solution.py:113
  82.9 12.9 %all-reduce.19 = (f32[]{:T(128)}, f32[1]{0:T(128)}) all-reduce(f32[]{:T(128)} %get-tuple-element.157, f32[1]{0:T(128)} %get-tuple-element.158), channel_id=1, replica_groups=mesh['gx'=8,'gy'=4] {'gy'}, use_global_device_ids=true, to_apply=%region_11.0 | all-reduce | flops 2 | bytes 16 | tf_op jit(solution)/shard_map/psum | solution.py:113
  101.1 3.0 collective-permute-start.5
  109.1 4.5 collective-permute-start.7
  122.3 12.4 %all-reduce.8 = (f32[]{:T(128)}, f32[2]{0:T(128)S(1)}) all-reduce(f32[]{:T(128)S(6)} %add.689, f32[2]{0:T(128)S(1)} %pad_maximum_fusion.120), channel_id=1, replica_groups=mesh['gx'=8,'gy'=4] {'gx'}, use_global_device_ids=true, to_apply=%region_21.0 | all-reduce | flops 3 | bytes 24 | tf_op jit(solution)/shard_map/psum | solution.py:113
  134.7 11.3 %all-reduce.18 = (f32[]{:T(128)}, f32[2]{0:T(128)S(1)}) all-reduce(f32[]{:T(128)} %get-tuple-element.155, f32[2]{0:T(128)S(1)} %get-tuple-element.156), channel_id=1, replica_groups=mesh['gx'=8,'gy'=4] {'gy'}, use_global_device_ids=true, to_apply=%region_22.0 | all-reduce | flops 3 | bytes 24 | tf_op jit(solution)/shard_map/psum | solution.py:113
  153.7 3.0 collective-permute-start.9
  162.3 4.5 collective-permute-start.11
  177.6 12.4 %all-reduce.7 = (f32[]{:T(128)}, f32[3]{0:T(128)S(1)}) all-reduce(f32[]{:T(128)S(6)} %add.700, f32[3]{0:T(128)S(1)} %pad_maximum_fusion.121), channel_id=1, replica_groups=mesh['gx'=8,'gy'=4] {'gx'}, use_global_device_ids=true, to_apply=%region_35.0 | all-reduce | flops 4 | bytes 32 | tf_op jit(solution)/shard_map/psum | solution.py:113
  190.0 11.9 %all-reduce.17 = (f32[]{:T(128)}, f32[3]{0:T(128)S(1)}) all-reduce(f32[]{:T(128)} %get-tuple-element.153, f32[3]{0:T(128)S(1)} %get-tuple-element.154), channel_id=1, replica_groups=mesh['gx'=8,'gy'=4] {'gy'}, use_global_device_ids=true, to_apply=%region_36.0 | all-reduce | flops 4 | bytes 32 | tf_op jit(solution)/shard_map/psum | solution.py:113
  211.5 3.0 collective-permute-start.13
  221.2 4.5 collective-permute-start.15
  237.8 12.4 %all-reduce.6 = (f32[]{:T(128)}, f32[4]{0:T(128)S(1)}) all-reduce(f32[]{:T(128)S(6)} %add.712, f32[4]{0:T(128)S(1)} %pad_maximum_fusion.122), channel_id=1, replica_groups=mesh['gx'=8,'gy'=4] {'gx'}, use_global_device_ids=true, to_apply=%region_51.0 | all-reduce | flops 5 | bytes 40 | tf_op jit(solution)/shard_map/psum | solution.py:113
  250.2 11.4 %all-reduce.16 = (f32[]{:T(128)}, f32[4]{0:T(128)S(1)}) all-reduce(f32[]{:T(128)} %get-tuple-element.151, f32[4]{0:T(128)S(1)} %get-tuple-element.152), channel_id=1, replica_groups=mesh['gx'=8,'gy'=4] {'gy'}, use_global_device_ids=true, to_apply=%region_52.0 | all-reduce | flops 5 | bytes 40 | tf_op jit(solution)/shard_map/psum | solution.py:113
  285.1 4.5 collective-permute-start.19
  303.1 12.4 %all-reduce.5 = (f32[]{:T(128)}, f32[5]{0:T(128)S(1)}) all-reduce(f32[]{:T(128)S(6)} %add.725, f32[5]{0:T(128)S(1)} %stack.210), channel_id=1, replica_groups=mesh['gx'=8,'gy'=4] {'gx'}, use_global_device_ids=true, to_apply=%region_69.0 | all-reduce | flops 6 | bytes 48 | tf_op jit(solution)/shard_map/psum | solution.py:113
  315.4 11.4 %all-reduce.15 = (f32[]{:T(128)}, f32[5]{0:T(128)S(1)}) all-reduce(f32[]{:T(128)} %get-tuple-element.149, f32[5]{0:T(128)S(1)} %get-tuple-element.150), channel_id=1, replica_groups=mesh['gx'=8,'gy'=4] {'gy'}, use_global_device_ids=true, to_apply=%region_70.0 | all-reduce | flops 6 | bytes 48 | tf_op jit(solution)/shard_map/psum | solution.py:113
  329.4 3.2 subtract_divide_fusion.13
  333.8 3.2 subtract_divide_fusion.4
  352.7 4.5 collective-permute-start.23
  371.9 12.4 %all-reduce.4 = (f32[]{:T(128)}, f32[6]{0:T(128)S(1)}) all-reduce(f32[]{:T(128)S(6)} %add.739, f32[6]{0:T(128)S(1)} %stack.217), channel_id=1, replica_groups=mesh['gx'=8,'gy'=4] {'gx'}, use_global_device_ids=true, to_apply=%region_89.0 | all-reduce | flops 7 | bytes 56 | tf_op jit(solution)/shard_map/psum | solution.py:113
  384.3 11.5 %all-reduce.14 = (f32[]{:T(128)}, f32[6]{0:T(128)S(1)}) all-reduce(f32[]{:T(128)} %get-tuple-element.147, f32[6]{0:T(128)S(1)} %get-tuple-element.148), channel_id=1, replica_groups=mesh['gx'=8,'gy'=4] {'gy'}, use_global_device_ids=true, to_apply=%region_90.0 | all-reduce | flops 7 | bytes 56 | tf_op jit(solution)/shard_map/psum | solution.py:113
  398.5 3.7 subtract_divide_fusion.12
  404.1 3.8 subtract_divide_fusion.3
  427.9 4.5 collective-permute-start.27
  449.2 12.4 %all-reduce.3 = (f32[]{:T(128)}, f32[7]{0:T(128)S(1)}) all-reduce(f32[]{:T(128)S(6)} %add.754, f32[7]{0:T(128)S(1)} %stack.225), channel_id=1, replica_groups=mesh['gx'=8,'gy'=4] {'gx'}, use_global_device_ids=true, to_apply=%region_111.0 | all-reduce | flops 8 | bytes 64 | tf_op jit(solution)/shard_map/psum | solution.py:113
  461.6 11.4 %all-reduce.13 = (f32[]{:T(128)}, f32[7]{0:T(128)S(1)}) all-reduce(f32[]{:T(128)} %get-tuple-element.145, f32[7]{0:T(128)S(1)} %get-tuple-element.146), channel_id=1, replica_groups=mesh['gx'=8,'gy'=4] {'gy'}, use_global_device_ids=true, to_apply=%region_112.0 | all-reduce | flops 8 | bytes 64 | tf_op jit(solution)/shard_map/psum | solution.py:113
  475.7 4.4 subtract_divide_fusion.11
  482.1 4.5 subtract_divide_fusion.2
  495.1 3.6 collective-permute-start.29
  512.6 4.5 collective-permute-start.31
  539.0 12.4 %all-reduce.2 = (f32[]{:T(128)}, f32[8]{0:T(128)S(1)}) all-reduce(f32[]{:T(128)S(6)} %add.770, f32[8]{0:T(128)S(1)} %stack.234), channel_id=1, replica_groups=mesh['gx'=8,'gy'=4] {'gx'}, use_global_device_ids=true, to_apply=%region_135.0 | all-reduce | flops 9 | bytes 72 | tf_op jit(solution)/shard_map/psum | solution.py:113
  551.3 11.3 %all-reduce.12 = (f32[]{:T(128)}, f32[8]{0:T(128)S(1)}) all-reduce(f32[]{:T(128)} %get-tuple-element.143, f32[8]{0:T(128)S(1)} %get-tuple-element.144), channel_id=1, replica_groups=mesh['gx'=8,'gy'=4] {'gy'}, use_global_device_ids=true, to_apply=%region_136.0 | all-reduce | flops 9 | bytes 72 | tf_op jit(solution)/shard_map/psum | solution.py:113
  565.4 5.0 subtract_divide_fusion.10
  573.0 5.1 subtract_divide_fusion.1
  589.1 3.6 collective-permute-start.33
  606.0 4.8 collective-permute-start.35
  634.0 13.0 %all-reduce.1 = (f32[]{:T(128)}, f32[9]{0:T(128)S(1)}) all-reduce(f32[]{:T(128)S(6)} %add.787, f32[9]{0:T(128)S(1)} %stack.244), channel_id=1, replica_groups=mesh['gx'=8,'gy'=4] {'gx'}, use_global_device_ids=true, to_apply=%region_161.0 | all-reduce | flops 10 | bytes 80 | tf_op jit(solution)/shard_map/psum | solution.py:113
  647.0 10.6 %all-reduce.11 = (f32[]{:T(128)}, f32[9]{0:T(128)S(1)}) all-reduce(f32[]{:T(128)} %get-tuple-element.141, f32[9]{0:T(128)S(1)} %get-tuple-element.142), channel_id=1, replica_groups=mesh['gx'=8,'gy'=4] {'gy'}, use_global_device_ids=true, to_apply=%region_162.0 | all-reduce | flops 10 | bytes 80 | tf_op jit(solution)/shard_map/psum | solution.py:113
  660.2 5.7 subtract_divide_fusion.9
  668.5 6.6 subtract_divide_fusion
  687.6 3.6 collective-permute-start.37
  706.1 4.5 collective-permute-start.39
  735.7 12.9 %all-reduce = (f32[10]{0:T(128)S(1)}, f32[]{:T(128)}) all-reduce(f32[10]{0:T(128)S(1)} %stack.255, f32[]{:T(128)S(6)} %add.805), channel_id=1, replica_groups=mesh['gx'=8,'gy'=4] {'gx'}, use_global_device_ids=true, to_apply=%region_185.0 | all-reduce | flops 11 | bytes 88 | tf_op jit(solution)/shard_map/psum | solution.py:113
  748.6 10.8 %all-reduce.10 = (f32[10]{0:T(128)S(1)}, f32[]{:T(128)}) all-reduce(f32[10]{0:T(128)S(1)} %get-tuple-element.139, f32[]{:T(128)} %get-tuple-element.140), channel_id=1, replica_groups=mesh['gx'=8,'gy'=4] {'gy'}, use_global_device_ids=true, to_apply=%region_186.0 | all-reduce | flops 11 | bytes 88 | tf_op jit(solution)/shard_map/psum | solution.py:113
  (518 shorter events, 209.3 us)
Async XLA Ops:
  2.0 50.2 %copy-start = (f32[2,16,2048]{2,1,0:T(8,128)S(1)}, f32[2,16,2048]{2,1,0:T(8,128)}, u32[]{:S(2)}) copy-start(f32[2,16,2048]{2,1,0:T(8,128)} %param.5) | copy-start | bytes 786436
  47.9 8.4 %collective-permute-start = (f32[1,16,33]{1,0,2:T(1,128)S(1)}, f32[1,16,33]{1,0,2:T(1,128)S(1)}, u32[]{:S(2)}, u32[]{:S(2)}) collective-permute-start(f32[1,16,33]{1,0,2:T(1,128)S(1)} %get-tuple-element.352), channel_id=1, source_target_pairs={{4,0},{8,4},{12,8},{16,12},{20,16},{24,20},{28,24},{5,1},{9,5},{13... | collective-permute-start | bytes 6344 | tf_op jit(solution)/shard_map/ppermute | solution.py:23
  49.2 7.1 collective-permute-start.1
  56.4 6.2 collective-permute-start.2
  57.7 6.5 collective-permute-start.3
  99.8 7.8 collective-permute-start.4
  101.1 6.5 collective-permute-start.5
  107.8 6.8 collective-permute-start.6
  109.1 6.7 collective-permute-start.7
  152.4 8.4 %collective-permute-start.8 = (f32[1,16,33]{1,0,2:T(1,128)S(1)}, f32[1,16,33]{1,0,2:T(1,128)S(1)}, u32[]{:S(2)}, u32[]{:S(2)}) collective-permute-start(f32[1,16,33]{1,0,2:T(1,128)S(1)} %get-tuple-element.338), channel_id=1, source_target_pairs={{4,0},{8,4},{12,8},{16,12},{20,16},{24,20},{28,24},{5,1},{9,5},{13... | collective-permute-start | bytes 6344 | tf_op jit(solution)/shard_map/ppermute | solution.py:23
  153.7 7.1 collective-permute-start.9
  161.0 6.6 collective-permute-start.10
  162.3 7.0 collective-permute-start.11
  210.2 9.5 %collective-permute-start.12 = (f32[1,16,33]{1,0,2:T(1,128)S(1)}, f32[1,16,33]{1,0,2:T(1,128)S(1)}, u32[]{:S(2)}, u32[]{:S(2)}) collective-permute-start(f32[1,16,33]{1,0,2:T(1,128)S(1)} %get-tuple-element.331), channel_id=1, source_target_pairs={{4,0},{8,4},{12,8},{16,12},{20,16},{24,20},{28,24},{5,1},{9,5},{13... | collective-permute-start | bytes 6344 | tf_op jit(solution)/shard_map/ppermute | solution.py:23
  211.5 8.2 %collective-permute-start.13 = (f32[1,16,33]{1,0,2:T(1,128)S(1)}, f32[1,16,33]{1,0,2:T(1,128)S(1)}, u32[]{:S(2)}, u32[]{:S(2)}) collective-permute-start(f32[1,16,33]{1,0,2:T(1,128)S(1)} %get-tuple-element.330), channel_id=1, source_target_pairs={{0,4},{4,8},{8,12},{12,16},{16,20},{20,24},{24,28},{1,5},{5,9},{9,... | collective-permute-start | bytes 6344 | tf_op jit(solution)/shard_map/ppermute | solution.py:21
  219.9 6.7 collective-permute-start.14
  221.2 7.0 collective-permute-start.15
  271.9 11.7 %collective-permute-start.16 = (f32[1,16,33]{1,0,2:T(1,128)}, f32[1,16,33]{1,0,2:T(1,128)S(1)}, u32[]{:S(2)}, u32[]{:S(2)}) collective-permute-start(f32[1,16,33]{1,0,2:T(1,128)} %get-tuple-element.324), channel_id=1, source_target_pairs={{4,0},{8,4},{12,8},{16,12},{20,16},{24,20},{28,24},{5,1},{9,5},{13... | collective-permute-start | bytes 6344 | tf_op jit(solution)/shard_map/ppermute | solution.py:23
  273.2 10.4 %collective-permute-start.17 = (f32[1,16,33]{1,0,2:T(1,128)}, f32[1,16,33]{1,0,2:T(1,128)S(1)}, u32[]{:S(2)}, u32[]{:S(2)}) collective-permute-start(f32[1,16,33]{1,0,2:T(1,128)} %get-tuple-element.323), channel_id=1, source_target_pairs={{0,4},{4,8},{8,12},{12,16},{16,20},{20,24},{24,28},{1,5},{5,9},{9,... | collective-permute-start | bytes 6344 | tf_op jit(solution)/shard_map/ppermute | solution.py:21
  283.8 6.7 collective-permute-start.18
  285.1 7.0 collective-permute-start.19
  337.7 13.5 %collective-permute-start.20 = (f32[1,16,33]{1,0,2:T(1,128)S(1)}, f32[1,16,33]{1,0,2:T(1,128)S(1)}, u32[]{:S(2)}, u32[]{:S(2)}) collective-permute-start(f32[1,16,33]{1,0,2:T(1,128)S(1)} %get-tuple-element.317), channel_id=1, source_target_pairs={{4,0},{8,4},{12,8},{16,12},{20,16},{24,20},{28,24},{5,1},{9,5},{13... | collective-permute-start | bytes 6344 | tf_op jit(solution)/shard_map/ppermute | solution.py:23
  339.0 12.2 %collective-permute-start.21 = (f32[1,16,33]{1,0,2:T(1,128)S(1)}, f32[1,16,33]{1,0,2:T(1,128)S(1)}, u32[]{:S(2)}, u32[]{:S(2)}) collective-permute-start(f32[1,16,33]{1,0,2:T(1,128)S(1)} %get-tuple-element.316), channel_id=1, source_target_pairs={{0,4},{4,8},{8,12},{12,16},{16,20},{20,24},{24,28},{1,5},{5,9},{9,... | collective-permute-start | bytes 6344 | tf_op jit(solution)/shard_map/ppermute | solution.py:21
  351.4 6.7 collective-permute-start.22
  352.7 7.0 collective-permute-start.23
  411.2 15.2 %collective-permute-start.24 = (f32[1,16,33]{1,0,2:T(1,128)}, f32[1,16,33]{1,0,2:T(1,128)S(1)}, u32[]{:S(2)}, u32[]{:S(2)}) collective-permute-start(f32[1,16,33]{1,0,2:T(1,128)} %get-tuple-element.309), channel_id=1, source_target_pairs={{4,0},{8,4},{12,8},{16,12},{20,16},{24,20},{28,24},{5,1},{9,5},{13... | collective-permute-start | bytes 6344 | tf_op jit(solution)/shard_map/ppermute | solution.py:23
  412.5 13.9 %collective-permute-start.25 = (f32[1,16,33]{1,0,2:T(1,128)}, f32[1,16,33]{1,0,2:T(1,128)S(1)}, u32[]{:S(2)}, u32[]{:S(2)}) collective-permute-start(f32[1,16,33]{1,0,2:T(1,128)} %get-tuple-element.308), channel_id=1, source_target_pairs={{0,4},{4,8},{8,12},{12,16},{16,20},{20,24},{24,28},{1,5},{5,9},{9,... | collective-permute-start | bytes 6344 | tf_op jit(solution)/shard_map/ppermute | solution.py:21
  426.6 6.7 collective-permute-start.26
  427.9 7.0 collective-permute-start.27
  489.2 9.5 %copy-start.3 = (f32[2,16,32,1]{3,2,1,0:T(8,128)S(1)}, f32[2,16,32,1]{3,2,1,0:T(8,128)}, u32[]{:S(2)}) copy-start(f32[2,16,32,1]{3,2,1,0:T(8,128)} %get-tuple-element.217) | copy-start | bytes 12292
  493.8 16.6 %collective-permute-start.28 = (f32[1,16,33]{1,0,2:T(1,128)}, f32[1,16,33]{1,0,2:T(1,128)S(1)}, u32[]{:S(2)}, u32[]{:S(2)}) collective-permute-start(f32[1,16,33]{1,0,2:T(1,128)} %get-tuple-element.300), channel_id=1, source_target_pairs={{4,0},{8,4},{12,8},{16,12},{20,16},{24,20},{28,24},{5,1},{9,5},{13... | collective-permute-start | bytes 6344 | tf_op jit(solution)/shard_map/ppermute | solution.py:23
  495.1 15.3 %collective-permute-start.29 = (f32[1,16,33]{1,0,2:T(1,128)}, f32[1,16,33]{1,0,2:T(1,128)}, u32[]{:S(2)}, u32[]{:S(2)}) collective-permute-start(f32[1,16,33]{1,0,2:T(1,128)} %get-tuple-element.299), channel_id=1, source_target_pairs={{0,4},{4,8},{8,12},{12,16},{16,20},{20,24},{24,28},{1,5},{5,9},{9,... | collective-permute-start | bytes 6344 | tf_op jit(solution)/shard_map/ppermute | solution.py:21
  501.9 7.6 copy-start.8
  511.3 7.0 collective-permute-start.30
  512.6 6.5 collective-permute-start.31
  565.4 7.6 copy-start.19
  580.7 12.0 %copy-start.2 = (f32[2,16,32,1]{3,2,1,0:T(8,128)S(1)}, f32[2,16,32,1]{3,2,1,0:T(8,128)}, u32[]{:S(2)}) copy-start(f32[2,16,32,1]{3,2,1,0:T(8,128)} %get-tuple-element.213) | copy-start | bytes 12292
  587.8 16.0 %collective-permute-start.32 = (f32[1,16,33]{1,0,2:T(1,128)}, f32[1,16,33]{1,0,2:T(1,128)}, u32[]{:S(2)}, u32[]{:S(2)}) collective-permute-start(f32[1,16,33]{1,0,2:T(1,128)} %get-tuple-element.290), channel_id=1, source_target_pairs={{4,0},{8,4},{12,8},{16,12},{20,16},{24,20},{28,24},{5,1},{9,5},{13... | collective-permute-start | bytes 6344 | tf_op jit(solution)/shard_map/ppermute | solution.py:23
  589.1 14.7 %collective-permute-start.33 = (f32[1,16,33]{1,0,2:T(1,128)}, f32[1,16,33]{1,0,2:T(1,128)}, u32[]{:S(2)}, u32[]{:S(2)}) collective-permute-start(f32[1,16,33]{1,0,2:T(1,128)} %get-tuple-element.289), channel_id=1, source_target_pairs={{0,4},{4,8},{8,12},{12,16},{16,20},{20,24},{24,28},{1,5},{5,9},{9,... | collective-permute-start | bytes 6344 | tf_op jit(solution)/shard_map/ppermute | solution.py:21
  595.9 7.0 copy-start.7
  604.7 7.9 %collective-permute-start.34 = (f32[4,1,33]{1,0,2:T(4,128)S(1)}, f32[4,1,33]{1,0,2:T(4,128)S(1)}, u32[]{:S(2)}, u32[]{:S(2)}) collective-permute-start(f32[4,1,33]{1,0,2:T(4,128)S(1)} %get-tuple-element.250), channel_id=1, source_target_pairs={{1,0},{2,1},{3,2},{5,4},{6,5},{7,6},{9,8},{10,9},{11,10},{13,12},{... | collective-permute-start | bytes 1592 | tf_op jit(solution)/shard_map/ppermute | solution.py:23
  606.0 6.6 collective-permute-start.35
  634.0 26.2 %copy-start.24 = (f32[2,16,32]{1,0,2:T(2,128)S(1)}, f32[2,16,32]{1,0,2:T(2,128)}, u32[]{:S(2)}) copy-start(f32[2,16,32]{1,0,2:T(2,128)} %get-tuple-element.181) | copy-start | bytes 12292
  678.6 12.7 %copy-start.1 = (f32[2,16,32,1]{3,2,1,0:T(8,128)S(1)}, f32[2,16,32,1]{3,2,1,0:T(8,128)}, u32[]{:S(2)}) copy-start(f32[2,16,32,1]{3,2,1,0:T(8,128)} %get-tuple-element.209) | copy-start | bytes 12292
  686.4 17.0 %collective-permute-start.36 = (f32[1,16,33]{1,0,2:T(1,128)}, f32[1,16,33]{1,0,2:T(1,128)}, u32[]{:S(2)}, u32[]{:S(2)}) collective-permute-start(f32[1,16,33]{1,0,2:T(1,128)} %get-tuple-element.279), channel_id=1, source_target_pairs={{4,0},{8,4},{12,8},{16,12},{20,16},{24,20},{28,24},{5,1},{9,5},{13... | collective-permute-start | bytes 6344 | tf_op jit(solution)/shard_map/ppermute | solution.py:23
  687.6 15.7 %collective-permute-start.37 = (f32[1,16,33]{1,0,2:T(1,128)}, f32[1,16,33]{1,0,2:T(1,128)}, u32[]{:S(2)}, u32[]{:S(2)}) collective-permute-start(f32[1,16,33]{1,0,2:T(1,128)} %get-tuple-element.278), channel_id=1, source_target_pairs={{0,4},{4,8},{8,12},{12,16},{16,20},{20,24},{24,28},{1,5},{5,9},{9,... | collective-permute-start | bytes 6344 | tf_op jit(solution)/shard_map/ppermute | solution.py:21
  704.8 7.7 collective-permute-start.38
  706.1 6.5 collective-permute-start.39
  (55 other events, 92.2 us)
